TPU v7x, 32 devices: a whole 2x2x4 slice. The times are simulated.
32 devices in a mesh: band: 32 (over z, y, x, core).
Axes of the slice: x: 2, y: 2, z: 4, core: 2. Of those that a mesh axis runs over, the one named last changes fastest.
Arguments:
- jones_start: float32 [32, 32, 512], P('band'), may hold values from -1.5 to 1.5
- visible: bfloat16 [32, 8, 4096], P('band'), may hold values from -6 to 6
- coherent: bfloat16 [32, 32, 4096], P('band'), may hold values from -1 to 1
- stations: int32 [2, 4096], replicated, may hold values from 0 to 511, as said below
- weights: float32 [32, 512], P('band'), may hold values from 0.2 to 2
- multiplier_start: float32 [32, 32, 512], P('band'), may hold values from -2 to 2
Outputs:
- jones_final: float32 [32, 32, 512], P('band')
- multiplier_final: float32 [32, 32, 512], P('band')
- coefficients: float32 [96, 512], P(None, 'band')
Inputs may be any that keep to these rules, and one draw needn't show every extreme that they name: Rows 0 and 1 of each column name two different stations; the same baselines serve every subband.
All inputs are finite; a program needn't handle non-finite values.
Results may differ from a plain program's by a relative error of at most 0.0003.
Values sent between devices are 32-bit elements; how exact they have to be, the bound alone decides.
A program may use at most 64 MiB of HBM per device.

v0:
```python
import jax
import jax.numpy as jnp
from jax import lax
from jax.sharding import PartitionSpec as P

ITERS = 2
PENALTY = 1.0
STEP_SIZE = 0.05
PAIR_LIST = ((0, 0), (0, 1), (0, 2), (1, 1), (1, 2), (2, 2))


def matrix_product(first_real, first_imag, second_real, second_imag):

    def contract(lhs_part, rhs_part):
        return jnp.sum(lhs_part[:, :, :, None, :] * rhs_part[:, None, :, :, :], axis=2)

    real_part = contract(first_real, second_real) - contract(first_imag, second_imag)
    imag_part = contract(first_real, second_imag) + contract(first_imag, second_real)
    return (real_part, imag_part)


def band_loss(
    jones_band, visible_band, coherent_band, stations, target_band, multiplier_band, weight_band
):
    baseline_count = stations.shape[1]
    direction_count = jones_band.shape[0] // 8
    station_first = jnp.take(jones_band, stations[0], axis=1).reshape(
        direction_count, 2, 2, 2, baseline_count
    )
    station_second = jnp.take(jones_band, stations[1], axis=1).reshape(
        direction_count, 2, 2, 2, baseline_count
    )
    sky_model = coherent_band.astype(jnp.float32).reshape(direction_count, 2, 2, 2, baseline_count)
    inner_real, inner_imag = matrix_product(
        station_first[:, 0], station_first[:, 1], sky_model[:, 0], sky_model[:, 1]
    )
    herm_real = jnp.swapaxes(station_second[:, 0], 1, 2)
    herm_imag = -jnp.swapaxes(station_second[:, 1], 1, 2)
    model_real, model_imag = matrix_product(inner_real, inner_imag, herm_real, herm_imag)
    predicted = jnp.stack([jnp.sum(model_real, axis=0), jnp.sum(model_imag, axis=0)])
    misfit = visible_band.astype(jnp.float32).reshape(2, 2, 2, baseline_count) - predicted
    data_scale = jones_band.shape[1] / (2.0 * baseline_count)
    distance = jones_band - target_band
    return (
        data_scale * jnp.sum(misfit * misfit)
        + jnp.sum(multiplier_band * distance)
        + 0.5 * PENALTY * jnp.sum(weight_band[None, :] * distance * distance)
    )


def descend(
    jones_band, visible_band, coherent_band, stations, target_band, multiplier_band, weight_band
):
    slope_fn = jax.grad(band_loss)
    slope = slope_fn(
        jones_band, visible_band, coherent_band, stations, target_band, multiplier_band, weight_band
    )
    jones_band = jones_band - STEP_SIZE * slope
    return jones_band


def solve_normal(normal_matrix, right_side):
    gram_aa, gram_ab, gram_ac, gram_bb, gram_bc, gram_cc = [
        normal_matrix[position] for position in range(6)
    ]
    cofac_aa = gram_bb * gram_cc - gram_bc * gram_bc
    cofac_ab = gram_ac * gram_bc - gram_ab * gram_cc
    cofac_ac = gram_ab * gram_bc - gram_ac * gram_bb
    cofac_bb = gram_aa * gram_cc - gram_ac * gram_ac
    cofac_bc = gram_ab * gram_ac - gram_aa * gram_bc
    cofac_cc = gram_aa * gram_bb - gram_ab * gram_ab
    determinant = gram_aa * cofac_aa + gram_ab * cofac_ab + gram_ac * cofac_ac
    inverse_det = 1.0 / determinant
    first_term = right_side[0]
    second_term = right_side[1]
    third_term = right_side[2]
    coeff_a = (cofac_aa * first_term + cofac_ab * second_term + cofac_ac * third_term) * inverse_det
    coeff_b = (cofac_ab * first_term + cofac_bb * second_term + cofac_bc * third_term) * inverse_det
    coeff_c = (cofac_ac * first_term + cofac_bc * second_term + cofac_cc * third_term) * inverse_det
    return jnp.stack([coeff_a, coeff_b, coeff_c])


def local(jones_start, visible, coherent, stations, weights, multiplier_start):
    band_count = lax.axis_size("band")
    band_index = lax.axis_index("band")
    abscissa = -1.0 + 2.0 * band_index.astype(jnp.float32) / (band_count - 1)
    basis_local = (jnp.ones((), jnp.float32), abscissa, 1.5 * abscissa * abscissa - 0.5)
    weight_band = weights[0]
    visible_band = visible[0]
    coherent_band = coherent[0]
    station_share = weights.shape[1] // band_count
    products = jnp.stack(
        [basis_local[first_idx] * basis_local[second_idx] for first_idx, second_idx in PAIR_LIST]
    )
    normal_term = PENALTY * products[:, None] * weight_band[None, :]
    normal_solver = lax.psum(normal_term, "band")

    def iteration(turn_index, carried):
        jones_band, multiplier_band, owned_prior = carried
        combined = multiplier_band + PENALTY * weight_band[None, :] * jones_band
        weighted_terms = jnp.stack([basis_local[term_index] * combined for term_index in range(3)])
        full_sums = lax.psum(weighted_terms, "band")
        coefficients = solve_normal(normal_solver, full_sums)
        owned_coeff = lax.dynamic_slice_in_dim(
            coefficients, band_index * station_share, station_share, 2
        )
        target_band = (
            basis_local[0] * coefficients[0]
            + basis_local[1] * coefficients[1]
            + basis_local[2] * coefficients[2]
        )
        multiplier_band = multiplier_band + PENALTY * weight_band[None, :] * (
            jones_band - target_band
        )
        jones_band = descend(
            jones_band,
            visible_band,
            coherent_band,
            stations,
            target_band,
            multiplier_band,
            weight_band,
        )
        return (jones_band, multiplier_band, owned_coeff)

    owned_start = jnp.zeros((3, jones_start.shape[1], station_share), jnp.float32)
    jones_band, multiplier_band, owned_coeff = lax.fori_loop(
        0, ITERS, iteration, (jones_start[0], multiplier_start[0], owned_start)
    )
    coeff_rows = owned_coeff.reshape(
        owned_coeff.shape[0] * owned_coeff.shape[1], owned_coeff.shape[2]
    )
    return (jones_band[None], multiplier_band[None], coeff_rows)


def solution(mesh):
    return jax.shard_map(
        local,
        mesh=mesh,
        in_specs=(
            P("band", None, None),
            P("band", None, None),
            P("band", None, None),
            P(),
            P("band", None),
            P("band", None, None),
        ),
        out_specs=(P("band", None, None), P("band", None, None), P(None, "band")),
        check_vma=False,
    )
```

profile of v0, /device:TPU:8, one launch (start us, length us, event | category | flops | bytes accessed | tf_op | source)
XLA Modules:
  0.0 373.0 jit_solution(7236217893154198396)
XLA Ops:
  9.7 40.5 %psum.17 = f32[6,512]{1,0:T(8,128)S(1)} all-reduce(f32[6,512]{1,0:T(8,128)S(1)} %broadcast_multiply_fusion.1), channel_id=1, replica_groups=mesh['band'=32] {'band'}, use_global_device_ids=true, to_apply=%region_0.0 | all-reduce | flops 3072 | bytes 24576 | tf_op jit(solution)/shard_map/psum | solution.py:96
  50.8 313.9 %while.17 = (s32[]{:T(128)}, f32[32,512]{1,0:T(8,128)S(1)}, f32[32,512]{1,0:T(8,128)S(1)}, f32[3,32,16]{2,1,0:T(8,128)}, f32[1,512]{1,0:T(1,128)}, /*index=5*/f3...) while((s32[]{:T(128)}, f32[32,512]{1,0:T(8,128)S(1)}, ...), condition=%wide.region_27.0_spmd, body=%wide.region_1.28_spmd.sunk | while | flops 6967298 | bytes 52347996 | solution.py:127
  53.8 14.1 %gather_fusion.1 = f32[4096,32]{1,0:T(8,128)} fusion(f32[32,512]{0,1:T(8,128)S(1)} %copy.101, s32[4096]{0:T(1024)S(1)} %get-tuple-element.581), kind=kCustom, calls=%fused_computation.1.clone.clone.1 | custom fusion | bytes 1064960 | tf_op jit(solution)/shard_map/while/body/eval_jaxpr/jvp(jit(_take))/gather | solution.py:27
  67.9 3.6 select_bitcast_fusion.5
  72.5 0.9 copy.106
  75.0 14.1 %gather_fusion = f32[4096,32]{1,0:T(8,128)} fusion(f32[32,512]{0,1:T(8,128)S(1)} %copy.101, s32[4096]{0:T(1024)S(1)} %get-tuple-element.578), kind=kCustom, calls=%fused_computation.clone.clone.1 | custom fusion | bytes 1064960 | tf_op jit(solution)/shard_map/while/body/eval_jaxpr/jvp(jit(_take))/gather | solution.py:30
  89.1 3.6 select_bitcast_fusion.4
  96.4 1.3 multiply_reduce_fusion.26
  100.1 2.0 copy.114
  103.5 22.7 %scatter_custom_fusion.8 = f32[32,512]{0,1:T(8,128)S(1)} fusion(s32[4096]{0:T(1024)} %get-tuple-element.603, f32[4096,32]{1,0:T(8,128)} %copy.114, f32[]{:T(128)} %constant.70.clone.25..sunk), kind=kCustom, calls=%fused_computation.50.clone.1 | custom fusion | flops 131072 | bytes 66048 | tf_op jit(solution)/shard_map/while/body/eval_jaxpr/transpose(jvp(jit(_take)))/scatter-add | solution.py:27
  126.2 57.3 %all-reduce.6.cloned.1.call-done = f32[3,32,512]{2,1,0:T(8,128)} async-done(((f32[3,32,512]{2,1,0:T(8,128)}), f32[3,32,512]{2,1,0:T(8,128)}) %all-reduce.6.cloned.1.call-update) | async-done | bytes 196624 | tf_op jit(solution)/shard_map/while/body/eval_jaxpr/psum | solution.py:102
  183.5 1.0 add_add_fusion.2
  184.7 22.5 %scatter_fusion = f32[32,512]{0,1:T(8,128)S(1)} fusion(f32[32,512]{0,1:T(8,128)S(1)} %copy.102, s32[4096]{0:T(1024)S(1)} %get-tuple-element.577, f32[4096,32]{1,0:T(8,128)S(1)} %copy.112), kind=kCustom, calls=%fused_computation.2.clone.1 | custom fusion | flops 131072 | bytes 1589248 | tf_op jit(solution)/shard_map/while/body/eval_jaxpr/transpose(jvp(jit(_take)))/scatter-add | solution.py:30
  211.2 14.1 %gather_fusion.1 = f32[4096,32]{1,0:T(8,128)} fusion(f32[32,512]{0,1:T(8,128)S(1)} %copy.101, s32[4096]{0:T(1024)S(1)} %get-tuple-element.581), kind=kCustom, calls=%fused_computation.1.clone.clone.1 | custom fusion | bytes 1064960 | tf_op jit(solution)/shard_map/while/body/eval_jaxpr/jvp(jit(_take))/gather | solution.py:27
  225.3 3.6 select_bitcast_fusion.5
  232.3 14.1 %gather_fusion = f32[4096,32]{1,0:T(8,128)} fusion(f32[32,512]{0,1:T(8,128)S(1)} %copy.101, s32[4096]{0:T(1024)S(1)} %get-tuple-element.578), kind=kCustom, calls=%fused_computation.clone.clone.1 | custom fusion | bytes 1064960 | tf_op jit(solution)/shard_map/while/body/eval_jaxpr/jvp(jit(_take))/gather | solution.py:30
  246.4 3.6 select_bitcast_fusion.4
  253.8 1.3 multiply_reduce_fusion.26
  257.4 2.0 copy.114
  260.8 22.7 %scatter_custom_fusion.8 = f32[32,512]{0,1:T(8,128)S(1)} fusion(s32[4096]{0:T(1024)} %get-tuple-element.603, f32[4096,32]{1,0:T(8,128)} %copy.114, f32[]{:T(128)} %constant.70.clone.25..sunk), kind=kCustom, calls=%fused_computation.50.clone.1 | custom fusion | flops 131072 | bytes 66048 | tf_op jit(solution)/shard_map/while/body/eval_jaxpr/transpose(jvp(jit(_take)))/scatter-add | solution.py:27
  283.5 56.6 %all-reduce.6.cloned.1.call-done = f32[3,32,512]{2,1,0:T(8,128)} async-done(((f32[3,32,512]{2,1,0:T(8,128)}), f32[3,32,512]{2,1,0:T(8,128)}) %all-reduce.6.cloned.1.call-update) | async-done | bytes 196624 | tf_op jit(solution)/shard_map/while/body/eval_jaxpr/psum | solution.py:102
  340.1 1.0 add_add_fusion.2
  341.3 22.5 %scatter_fusion = f32[32,512]{0,1:T(8,128)S(1)} fusion(f32[32,512]{0,1:T(8,128)S(1)} %copy.102, s32[4096]{0:T(1024)S(1)} %get-tuple-element.577, f32[4096,32]{1,0:T(8,128)S(1)} %copy.112), kind=kCustom, calls=%fused_computation.2.clone.1 | custom fusion | flops 131072 | bytes 1589248 | tf_op jit(solution)/shard_map/while/body/eval_jaxpr/transpose(jvp(jit(_take)))/scatter-add | solution.py:30
  364.7 1.5 copy.85
  (171 shorter events, 31.7 us)
Async XLA Ops:
  50.8 132.8 %all-reduce.6.cloned.1.call-start = ((), (), s32[]{:S(2)}) async-start(), calls=%async_computation | async-start | bytes 393216 | tf_op jit(solution)/shard_map/while/body/eval_jaxpr/psum | solution.py:102
  72.1 2.1 copy-start.5
  93.3 1.1 copy-start.1
  95.1 1.3 copy-start.7
  102.4 81.1 %copy-start.8 = (f32[1,512]{1,0:T(1,128)S(1)}, f32[1,512]{1,0:T(1,128)}, u32[]{:S(2)}) copy-start(f32[1,512]{1,0:T(1,128)} %get-tuple-element.667) | copy-start | bytes 6148 | tf_op jit(solution)/shard_map/while
  102.4 81.1 %copy-start.9 = (f32[1,512]{1,0:T(1,128)S(1)}, f32[1,512]{1,0:T(1,128)}, u32[]{:S(2)}) copy-start(f32[1,512]{1,0:T(1,128)} %get-tuple-element.666) | copy-start | bytes 6148 | tf_op jit(solution)/shard_map/while
  102.4 81.1 %copy-start.10 = (f32[1,512]{1,0:T(1,128)S(1)}, f32[1,512]{1,0:T(1,128)}, u32[]{:S(2)}) copy-start(f32[1,512]{1,0:T(1,128)} %get-tuple-element.663) | copy-start | bytes 6148 | tf_op jit(solution)/shard_map/while
  102.5 81.1 %copy-start.11 = (f32[1,512]{1,0:T(1,128)S(1)}, f32[1,512]{1,0:T(1,128)}, u32[]{:S(2)}) copy-start(f32[1,512]{1,0:T(1,128)} %get-tuple-element.671) | copy-start | bytes 6148 | tf_op jit(solution)/shard_map/while
  102.5 81.1 %copy-start.12 = (f32[1,512]{1,0:T(1,128)S(1)}, f32[1,512]{1,0:T(1,128)}, u32[]{:S(2)}) copy-start(f32[1,512]{1,0:T(1,128)} %get-tuple-element.670) | copy-start | bytes 6148 | tf_op jit(solution)/shard_map/while
  102.5 81.1 %copy-start.13 = (f32[1,512]{1,0:T(1,128)S(1)}, f32[1,512]{1,0:T(1,128)}, u32[]{:S(2)}) copy-start(f32[1,512]{1,0:T(1,128)} %get-tuple-element.669) | copy-start | bytes 6148 | tf_op jit(solution)/shard_map/while
  184.7 22.7 %copy-start.2 = (f32[3,32,512]{2,1,0:T(8,128)S(1)}, f32[3,32,512]{2,1,0:T(8,128)}, u32[]{:S(2)}) copy-start(f32[3,32,512]{2,1,0:T(8,128)} %all-reduce.6.cloned.1.call-done) | copy-start | bytes 589828 | tf_op jit(solution)/shard_map/while
  208.1 132.0 %all-reduce.6.cloned.1.call-start = ((), (), s32[]{:S(2)}) async-start(), calls=%async_computation | async-start | bytes 393216 | tf_op jit(solution)/shard_map/while/body/eval_jaxpr/psum | solution.py:102
  229.4 2.1 copy-start.5
  250.6 1.1 copy-start.1
  252.5 1.3 copy-start.7
  259.8 80.3 %copy-start.8 = (f32[1,512]{1,0:T(1,128)S(1)}, f32[1,512]{1,0:T(1,128)}, u32[]{:S(2)}) copy-start(f32[1,512]{1,0:T(1,128)} %get-tuple-element.667) | copy-start | bytes 6148 | tf_op jit(solution)/shard_map/while
  259.8 80.3 %copy-start.9 = (f32[1,512]{1,0:T(1,128)S(1)}, f32[1,512]{1,0:T(1,128)}, u32[]{:S(2)}) copy-start(f32[1,512]{1,0:T(1,128)} %get-tuple-element.666) | copy-start | bytes 6148 | tf_op jit(solution)/shard_map/while
  259.8 80.3 %copy-start.10 = (f32[1,512]{1,0:T(1,128)S(1)}, f32[1,512]{1,0:T(1,128)}, u32[]{:S(2)}) copy-start(f32[1,512]{1,0:T(1,128)} %get-tuple-element.663) | copy-start | bytes 6148 | tf_op jit(solution)/shard_map/while
  259.8 80.3 %copy-start.11 = (f32[1,512]{1,0:T(1,128)S(1)}, f32[1,512]{1,0:T(1,128)}, u32[]{:S(2)}) copy-start(f32[1,512]{1,0:T(1,128)} %get-tuple-element.671) | copy-start | bytes 6148 | tf_op jit(solution)/shard_map/while
  259.8 80.3 %copy-start.12 = (f32[1,512]{1,0:T(1,128)S(1)}, f32[1,512]{1,0:T(1,128)}, u32[]{:S(2)}) copy-start(f32[1,512]{1,0:T(1,128)} %get-tuple-element.670) | copy-start | bytes 6148 | tf_op jit(solution)/shard_map/while
  259.8 80.3 %copy-start.13 = (f32[1,512]{1,0:T(1,128)S(1)}, f32[1,512]{1,0:T(1,128)}, u32[]{:S(2)}) copy-start(f32[1,512]{1,0:T(1,128)} %get-tuple-element.669) | copy-start | bytes 6148 | tf_op jit(solution)/shard_map/while
  341.3 22.7 %copy-start.2 = (f32[3,32,512]{2,1,0:T(8,128)S(1)}, f32[3,32,512]{2,1,0:T(8,128)}, u32[]{:S(2)}) copy-start(f32[3,32,512]{2,1,0:T(8,128)} %all-reduce.6.cloned.1.call-done) | copy-start | bytes 589828 | tf_op jit(solution)/shard_map/while
  364.7 1.5 copy-start.3
  364.7 1.5 copy-start.4
  (6 other events, 5.1 us)
Sparse Core Ops, SparseCore 0:
  57.1 126.3 all-reduce.5
  214.4 125.6 all-reduce.5
where the time goes:
time: 374 us; the launch traced here: 373 us
  other arithmetic  123 us (33%)
  waiting for transfers between devices  114 us (30%)
  local copies, waits for them, and re-layouts  80.8 us (22%)
  blocking collectives  40.5 us (11%)
  between operations  14 us (4%)
    psum x2, waiting for transfers between devices, iteration(): full_sums = lax.psum(weighted_terms, 'band')  114 us
    scatter-add x2, other arithmetic, band_loss(): jnp.take(jones_band, stations[0], axis=1)  45.4 us
    scatter-add x2, other arithmetic, band_loss(): jnp.take(jones_band, stations[1], axis=1)  45 us
    psum x1, blocking collectives, local(): normal_solver = lax.psum(normal_term, 'band')  40.5 us
    gather x2, local copies, waits for them, and re-layouts, band_loss(): jnp.take(jones_band, stations[0], axis=1)  28.2 us
    gather x2, local copies, waits for them, and re-layouts, band_loss(): jnp.take(jones_band, stations[1], axis=1)  28.2 us
    select_n x4, other arithmetic, band_loss(): jnp.take(jones_band, stations[0], axis=1)  8.44 us
  transfers between devices with their start and end apart: 2, of which 2 were waited for; matrix products, arithmetic and copies ran while one was open for 39% of the time, Pallas kernels for 0%

commit v1 on v0

--- a/solution.py
+++ b/solution.py
@@ -99,7 +99,7 @@
         jones_band, multiplier_band, owned_prior = carried
         combined = multiplier_band + PENALTY * weight_band[None, :] * jones_band
         weighted_terms = jnp.stack([basis_local[term_index] * combined for term_index in range(3)])
-        full_sums = lax.psum(weighted_terms, "band")
+        full_sums = jnp.sum(lax.all_gather(weighted_terms, "band"), axis=0)
         coefficients = solve_normal(normal_solver, full_sums)
         owned_coeff = lax.dynamic_slice_in_dim(
             coefficients, band_index * station_share, station_share, 2

time: 374 us -> 272 us (0.73)
  waiting for transfers between devices: 114 us -> 0.07 us
  other arithmetic: 123 us -> 129 us
    psum x2 -> x0, waiting for transfers between devices: 114 us -> none  [iteration(): full_sums = lax.psum(weighted_terms, 'band')]
    reduce_sum x0 -> x2, other arithmetic: none -> 6.8 us  [iteration(): full_sums = jnp.sum(lax.all_gather(weighted_terms, 'band'), axis=0)]
  transfers between devices with their start and end apart: 2 -> 2, of which waited for: 2 -> 0; matrix products, arithmetic and copies ran while one was open for 39% -> 56% of each run, Pallas kernels for 0% -> 0%
where the time goes in v1:
time: 272 us; the launch traced here: 269 us
  other arithmetic  129 us (47%)
  local copies, waits for them, and re-layouts  84.3 us (31%)
  blocking collectives  40.5 us (15%)
  between operations  14 us (5%)
    scatter-add x2, other arithmetic, band_loss(): jnp.take(jones_band, stations[0], axis=1)  45.4 us
    scatter-add x2, other arithmetic, band_loss(): jnp.take(jones_band, stations[1], axis=1)  45 us
    psum x1, blocking collectives, local(): normal_solver = lax.psum(normal_term, 'band')  40.5 us
    gather x2, local copies, waits for them, and re-layouts, band_loss(): jnp.take(jones_band, stations[0], axis=1)  28.2 us
    gather x2, local copies, waits for them, and re-layouts, band_loss(): jnp.take(jones_band, stations[1], axis=1)  28.1 us
    select_n x4, other arithmetic, band_loss(): jnp.take(jones_band, stations[0], axis=1)  8.43 us
    select_n x2, other arithmetic, band_loss(): jnp.take(jones_band, stations[1], axis=1)  7.23 us
    reduce_sum x2, other arithmetic, iteration(): full_sums = jnp.sum(lax.all_gather(weighted_terms, 'band'), axis=0)  6.8 us
  transfers between devices with their start and end apart: 2, of which 0 were waited for; matrix products, arithmetic and copies ran while one was open for 56% of the time, Pallas kernels for 0%

profile of v1, /device:TPU:8, one launch (start us, length us, event | category | flops | bytes accessed | tf_op | source)
XLA Modules:
  0.0 269.1 jit_solution(15739374982398202927)
XLA Ops:
  9.7 40.5 %psum.7 = f32[6,512]{1,0:T(8,128)S(1)} all-reduce(f32[6,512]{1,0:T(8,128)S(1)} %broadcast_multiply_fusion.1), channel_id=1, replica_groups=mesh['band'=32] {'band'}, use_global_device_ids=true, to_apply=%region_0.0 | all-reduce | flops 3072 | bytes 24576 | tf_op jit(solution)/shard_map/psum | solution.py:96
  50.8 210.0 %while.17 = (s32[]{:T(128)}, f32[32,512]{1,0:T(8,128)S(1)}, f32[32,512]{1,0:T(8,128)S(1)}, f32[3,32,16]{2,1,0:T(8,128)}, f32[1,512]{1,0:T(1,128)}, /*index=5*/f3...) while((s32[]{:T(128)}, f32[32,512]{1,0:T(8,128)S(1)}, ...), condition=%wide.region_27.0_spmd, body=%wide.region_1.28_spmd.sunk | while | flops 8441858 | bytes 75875416 | solution.py:127
  53.8 1.3 reshape.304
  55.2 14.1 %gather_fusion.1 = f32[4096,32]{1,0:T(8,128)} fusion(f32[32,512]{0,1:T(8,128)S(1)} %copy.126, s32[4096]{0:T(1024)S(1)} %get-tuple-element.581), kind=kCustom, calls=%fused_computation.1.clone.clone.1 | custom fusion | bytes 1064960 | tf_op jit(solution)/shard_map/while/body/eval_jaxpr/jvp(jit(_take))/gather | solution.py:27
  69.3 3.6 %select_bitcast_fusion.5 = f32[32,4096]{0,1:T(8,128)S(1)} fusion(f32[4096,32]{1,0:T(8,128)} %gather_fusion.1, pred[4096]{0:T(1024)(128)(4,1)S(1)} %compare_and_fusion.5), kind=kLoop, calls=%fused_computation.4.clone.1 | loop fusion | flops 131072 | bytes 1052672 | tf_op jit(solution)/shard_map/while/body/eval_jaxpr/jvp(jit(_take))/select_n | solution.py:27
  75.4 0.9 copy.131
  77.8 14.1 %gather_fusion = f32[4096,32]{1,0:T(8,128)} fusion(f32[32,512]{0,1:T(8,128)S(1)} %copy.126, s32[4096]{0:T(1024)S(1)} %get-tuple-element.578), kind=kCustom, calls=%fused_computation.clone.clone.1 | custom fusion | bytes 1064960 | tf_op jit(solution)/shard_map/while/body/eval_jaxpr/jvp(jit(_take))/gather | solution.py:30
  91.8 3.6 %select_bitcast_fusion.4 = f32[32,4096]{0,1:T(8,128)S(1)} fusion(f32[4096,32]{1,0:T(8,128)} %gather_fusion, pred[4096]{0:T(1024)(128)(4,1)S(1)} %compare_and_fusion.4), kind=kLoop, calls=%fused_computation.5.clone.1 | loop fusion | flops 131072 | bytes 1052672 | tf_op jit(solution)/shard_map/while/body/eval_jaxpr/jvp(jit(_take))/select_n | solution.py:30
  99.2 1.3 multiply_reduce_fusion.26
  103.2 2.0 copy.139
  105.8 22.7 %scatter_custom_fusion.8 = f32[32,512]{0,1:T(8,128)S(1)} fusion(s32[4096]{0:T(1024)} %get-tuple-element.603, f32[4096,32]{1,0:T(8,128)} %copy.139, f32[]{:T(128)} %constant.68.clone.25..sunk), kind=kCustom, calls=%fused_computation.50.clone.1 | custom fusion | flops 131072 | bytes 66048 | tf_op jit(solution)/shard_map/while/body/eval_jaxpr/transpose(jvp(jit(_take)))/scatter-add | solution.py:27
  128.6 3.4 %reduce_sum.357 = f32[3,32,512]{2,1,0:T(8,128)S(1)} reduce(f32[32,3,32,512]{3,2,1,0:T(8,128)} %bitcast.199, f32[]{:T(128)} %constant.68.clone.25..sunk), dimensions={0}, to_apply=%region_2.0 | reduce | flops 1523712 | bytes 6488068 | tf_op jit(solution)/shard_map/while/body/eval_jaxpr/reduce_sum | solution.py:102
  132.4 22.5 %scatter_fusion = f32[32,512]{0,1:T(8,128)S(1)} fusion(f32[32,512]{0,1:T(8,128)S(1)} %copy.127, s32[4096]{0:T(1024)S(1)} %copy-done.5, f32[4096,32]{1,0:T(8,128)S(1)} %copy.137), kind=kCustom, calls=%fused_computation.2.clone.1 | custom fusion | flops 131072 | bytes 1589248 | tf_op jit(solution)/shard_map/while/body/eval_jaxpr/transpose(jvp(jit(_take)))/scatter-add | solution.py:30
  158.8 1.3 reshape.304
  160.2 14.1 %gather_fusion.1 = f32[4096,32]{1,0:T(8,128)} fusion(f32[32,512]{0,1:T(8,128)S(1)} %copy.126, s32[4096]{0:T(1024)S(1)} %get-tuple-element.581), kind=kCustom, calls=%fused_computation.1.clone.clone.1 | custom fusion | bytes 1064960 | tf_op jit(solution)/shard_map/while/body/eval_jaxpr/jvp(jit(_take))/gather | solution.py:27
  174.2 3.6 %select_bitcast_fusion.5 = f32[32,4096]{0,1:T(8,128)S(1)} fusion(f32[4096,32]{1,0:T(8,128)} %gather_fusion.1, pred[4096]{0:T(1024)(128)(4,1)S(1)} %compare_and_fusion.5), kind=kLoop, calls=%fused_computation.4.clone.1 | loop fusion | flops 131072 | bytes 1052672 | tf_op jit(solution)/shard_map/while/body/eval_jaxpr/jvp(jit(_take))/select_n | solution.py:27
  182.7 14.1 %gather_fusion = f32[4096,32]{1,0:T(8,128)} fusion(f32[32,512]{0,1:T(8,128)S(1)} %copy.126, s32[4096]{0:T(1024)S(1)} %get-tuple-element.578), kind=kCustom, calls=%fused_computation.clone.clone.1 | custom fusion | bytes 1064960 | tf_op jit(solution)/shard_map/while/body/eval_jaxpr/jvp(jit(_take))/gather | solution.py:30
  196.8 3.6 %select_bitcast_fusion.4 = f32[32,4096]{0,1:T(8,128)S(1)} fusion(f32[4096,32]{1,0:T(8,128)} %gather_fusion, pred[4096]{0:T(1024)(128)(4,1)S(1)} %compare_and_fusion.4), kind=kLoop, calls=%fused_computation.5.clone.1 | loop fusion | flops 131072 | bytes 1052672 | tf_op jit(solution)/shard_map/while/body/eval_jaxpr/jvp(jit(_take))/select_n | solution.py:30
  204.1 1.3 multiply_reduce_fusion.26
  208.2 2.0 copy.139
  210.7 22.7 %scatter_custom_fusion.8 = f32[32,512]{0,1:T(8,128)S(1)} fusion(s32[4096]{0:T(1024)} %get-tuple-element.603, f32[4096,32]{1,0:T(8,128)} %copy.139, f32[]{:T(128)} %constant.68.clone.25..sunk), kind=kCustom, calls=%fused_computation.50.clone.1 | custom fusion | flops 131072 | bytes 66048 | tf_op jit(solution)/shard_map/while/body/eval_jaxpr/transpose(jvp(jit(_take)))/scatter-add | solution.py:27
  233.6 3.4 %reduce_sum.357 = f32[3,32,512]{2,1,0:T(8,128)S(1)} reduce(f32[32,3,32,512]{3,2,1,0:T(8,128)} %bitcast.199, f32[]{:T(128)} %constant.68.clone.25..sunk), dimensions={0}, to_apply=%region_2.0 | reduce | flops 1523712 | bytes 6488068 | tf_op jit(solution)/shard_map/while/body/eval_jaxpr/reduce_sum | solution.py:102
  237.4 22.5 %scatter_fusion = f32[32,512]{0,1:T(8,128)S(1)} fusion(f32[32,512]{0,1:T(8,128)S(1)} %copy.127, s32[4096]{0:T(1024)S(1)} %copy-done.5, f32[4096,32]{1,0:T(8,128)S(1)} %copy.137), kind=kCustom, calls=%fused_computation.2.clone.1 | custom fusion | flops 131072 | bytes 1589248 | tf_op jit(solution)/shard_map/while/body/eval_jaxpr/transpose(jvp(jit(_take)))/scatter-add | solution.py:30
  260.7 1.5 copy.110
  (173 shorter events, 34.2 us)
Async XLA Ops:
  50.8 77.8 %all-gather.5.cloned.1.call-start = ((), (), s32[]{:S(2)}) async-start(), calls=%async_computation | async-start | bytes 6488064 | tf_op jit(solution)/shard_map/while/body/eval_jaxpr/all_gather | solution.py:102
  97.8 1.2 copy-start.3
  105.2 23.3 %copy-start.7 = (f32[1,512]{1,0:T(1,128)S(1)}, f32[1,512]{1,0:T(1,128)}, u32[]{:S(2)}) copy-start(f32[1,512]{1,0:T(1,128)} %get-tuple-element.662) | copy-start | bytes 6148 | tf_op jit(solution)/shard_map/while
  105.2 23.4 %copy-start.14 = (f32[1,512]{1,0:T(1,128)S(1)}, f32[1,512]{1,0:T(1,128)}, u32[]{:S(2)}) copy-start(f32[1,512]{1,0:T(1,128)} %get-tuple-element.668) | copy-start | bytes 6148 | tf_op jit(solution)/shard_map/while
  128.6 3.5 %copy-start.8 = (f32[1,512]{1,0:T(1,128)S(1)}, f32[1,512]{1,0:T(1,128)}, u32[]{:S(2)}) copy-start(f32[1,512]{1,0:T(1,128)} %get-tuple-element.667) | copy-start | bytes 6148 | tf_op jit(solution)/shard_map/while
  128.6 3.5 %copy-start.9 = (f32[1,512]{1,0:T(1,128)S(1)}, f32[1,512]{1,0:T(1,128)}, u32[]{:S(2)}) copy-start(f32[1,512]{1,0:T(1,128)} %get-tuple-element.666) | copy-start | bytes 6148 | tf_op jit(solution)/shard_map/while
  128.6 3.5 %copy-start.10 = (f32[1,512]{1,0:T(1,128)S(1)}, f32[1,512]{1,0:T(1,128)}, u32[]{:S(2)}) copy-start(f32[1,512]{1,0:T(1,128)} %get-tuple-element.663) | copy-start | bytes 6148 | tf_op jit(solution)/shard_map/while
  128.6 3.5 %copy-start.11 = (f32[1,512]{1,0:T(1,128)S(1)}, f32[1,512]{1,0:T(1,128)}, u32[]{:S(2)}) copy-start(f32[1,512]{1,0:T(1,128)} %get-tuple-element.671) | copy-start | bytes 6148 | tf_op jit(solution)/shard_map/while
  128.6 3.5 %copy-start.12 = (f32[1,512]{1,0:T(1,128)S(1)}, f32[1,512]{1,0:T(1,128)}, u32[]{:S(2)}) copy-start(f32[1,512]{1,0:T(1,128)} %get-tuple-element.670) | copy-start | bytes 6148 | tf_op jit(solution)/shard_map/while
  128.6 3.5 %copy-start.13 = (f32[1,512]{1,0:T(1,128)S(1)}, f32[1,512]{1,0:T(1,128)}, u32[]{:S(2)}) copy-start(f32[1,512]{1,0:T(1,128)} %get-tuple-element.669) | copy-start | bytes 6148 | tf_op jit(solution)/shard_map/while
  128.6 3.8 %copy-start.5 = (s32[4096]{0:T(1024)S(1)}, s32[4096]{0:T(1024)}, u32[]{:S(2)}) copy-start(s32[4096]{0:T(1024)} %get-tuple-element.577) | copy-start | bytes 49156 | tf_op jit(solution)/shard_map/while
  155.7 77.8 %all-gather.5.cloned.1.call-start = ((), (), s32[]{:S(2)}) async-start(), calls=%async_computation | async-start | bytes 6488064 | tf_op jit(solution)/shard_map/while/body/eval_jaxpr/all_gather | solution.py:102
  202.8 1.2 copy-start.3
  210.1 23.3 %copy-start.7 = (f32[1,512]{1,0:T(1,128)S(1)}, f32[1,512]{1,0:T(1,128)}, u32[]{:S(2)}) copy-start(f32[1,512]{1,0:T(1,128)} %get-tuple-element.662) | copy-start | bytes 6148 | tf_op jit(solution)/shard_map/while
  210.1 23.4 %copy-start.14 = (f32[1,512]{1,0:T(1,128)S(1)}, f32[1,512]{1,0:T(1,128)}, u32[]{:S(2)}) copy-start(f32[1,512]{1,0:T(1,128)} %get-tuple-element.668) | copy-start | bytes 6148 | tf_op jit(solution)/shard_map/while
  233.5 3.5 %copy-start.8 = (f32[1,512]{1,0:T(1,128)S(1)}, f32[1,512]{1,0:T(1,128)}, u32[]{:S(2)}) copy-start(f32[1,512]{1,0:T(1,128)} %get-tuple-element.667) | copy-start | bytes 6148 | tf_op jit(solution)/shard_map/while
  233.6 3.5 %copy-start.9 = (f32[1,512]{1,0:T(1,128)S(1)}, f32[1,512]{1,0:T(1,128)}, u32[]{:S(2)}) copy-start(f32[1,512]{1,0:T(1,128)} %get-tuple-element.666) | copy-start | bytes 6148 | tf_op jit(solution)/shard_map/while
  233.6 3.5 %copy-start.10 = (f32[1,512]{1,0:T(1,128)S(1)}, f32[1,512]{1,0:T(1,128)}, u32[]{:S(2)}) copy-start(f32[1,512]{1,0:T(1,128)} %get-tuple-element.663) | copy-start | bytes 6148 | tf_op jit(solution)/shard_map/while
  233.6 3.5 %copy-start.11 = (f32[1,512]{1,0:T(1,128)S(1)}, f32[1,512]{1,0:T(1,128)}, u32[]{:S(2)}) copy-start(f32[1,512]{1,0:T(1,128)} %get-tuple-element.671) | copy-start | bytes 6148 | tf_op jit(solution)/shard_map/while
  233.6 3.5 %copy-start.12 = (f32[1,512]{1,0:T(1,128)S(1)}, f32[1,512]{1,0:T(1,128)}, u32[]{:S(2)}) copy-start(f32[1,512]{1,0:T(1,128)} %get-tuple-element.670) | copy-start | bytes 6148 | tf_op jit(solution)/shard_map/while
  233.6 3.5 %copy-start.13 = (f32[1,512]{1,0:T(1,128)S(1)}, f32[1,512]{1,0:T(1,128)}, u32[]{:S(2)}) copy-start(f32[1,512]{1,0:T(1,128)} %get-tuple-element.669) | copy-start | bytes 6148 | tf_op jit(solution)/shard_map/while
  233.6 3.8 %copy-start.5 = (s32[4096]{0:T(1024)S(1)}, s32[4096]{0:T(1024)}, u32[]{:S(2)}) copy-start(s32[4096]{0:T(1024)} %get-tuple-element.577) | copy-start | bytes 49156 | tf_op jit(solution)/shard_map/while
  260.7 1.5 copy-start.2
  260.7 1.5 copy-start.4
  (6 other events, 5.7 us)
Sparse Core Ops, SparseCore 0:
  54.4 69.0 all-gather.4
  159.4 69.0 all-gather.4
